TPU v7x, 512 devices: a whole 4x8x8 slice. The times are simulated.
512 devices in a mesh: grp: 8 (over z), limb: 64 (over x, y, core).
Axes of the slice: x: 4, y: 8, z: 8, core: 2. Of those that a mesh axis runs over, the one named last changes fastest.
Arguments:
- digits: float32 [32, 3, 16, 65536], P('grp', None, None, 'limb'), may hold values from 0 to 2047, as said below
- keys: float32 [32, 3, 2, 16, 65536], P('grp', None, None, None, 'limb'), may hold values from 0 to 2047, as said below
- requests: int32 [32, 32], P('grp'), may hold values from 0 to 1, as said below
- rotations: int32 [32], replicated, may hold values from 1 to 256, as said below
- moduli: int32 [16], replicated, may hold values from 2048 to 4095
Outputs:
- switched: float32 [32, 2, 16, 65536], P('grp', None, None, 'limb')
Inputs may be any that keep to these rules, and one draw needn't show every extreme that they name: `digits`: every entry is an integer. `keys`: every entry is an integer. `requests`: for each block of ciphertexts k * 4 to (k + 1) * 4 - 1 and each owner group's keys g * 4 to (g + 1) * 4 - 1, between 1 and 2 of those ciphertexts request one or more of those keys; in every draw some owner group is requested by exactly 2 ciphertexts of every block. `rotations`: the largest amount is exactly 256.
All inputs are finite; a program needn't handle non-finite values.
Results may differ from a plain program's by a relative error of at most 0.0003.
Values sent between devices are 32-bit elements; how exact they have to be, the bound alone decides.
A program may use at most 64 MiB of HBM per device.

v0:
```python
import jax
import jax.numpy as jnp
from jax import lax
from jax.sharding import PartitionSpec as P

RMAX = 256
CAP = 2


exact_mode = lax.Precision.HIGHEST


def from_behind(value, axis, steps):
    count = lax.axis_size(axis)
    pairs = [(source, (source + steps) % count) for source in range(count)]
    return lax.ppermute(value, axis, pairs)


def reduce_mod(amount, modulus):
    quotient = jnp.floor(amount * (1.0 / modulus))
    remainder = amount - quotient * modulus
    remainder = jnp.where(remainder < 0, remainder + modulus, remainder)
    return jnp.where(remainder >= modulus, remainder - modulus, remainder)


def per_device(digits, keys, requests, rotations, moduli):
    groups = lax.axis_size("grp")
    key_count = keys.shape[0]
    cipher_count = digits.shape[0]
    columns = digits.shape[-1]
    capacity = CAP
    widest = 2 * RMAX
    modulus = moduli.astype(jnp.float32)[:, None]
    wanted = requests.astype(jnp.float32).reshape(cipher_count, groups, key_count)
    needed = (jnp.sum(wanted, axis=2) > 0).astype(jnp.float32)
    rank_in = jnp.cumsum(needed, axis=0) - 1.0
    slot_index = jnp.arange(capacity, dtype=jnp.float32)
    chooser = needed.T[:, None, :] * (rank_in.T[:, None, :] == slot_index[None, :, None]).astype(
        jnp.float32
    )
    outgoing = jnp.einsum("hsc,cjlx->hsjlx", chooser, digits, precision=exact_mode)
    key_marks = jnp.einsum("hsc,chi->hsi", chooser, wanted, precision=exact_mode)
    amounts = 2 * lax.dynamic_slice_in_dim(rotations, lax.axis_index("grp") * key_count, key_count)
    position = jnp.arange(columns)
    incoming = lax.all_to_all(outgoing, "grp", split_axis=0, concat_axis=0, tiled=True)
    marks = lax.all_to_all(key_marks, "grp", split_axis=0, concat_axis=0, tiled=True)
    resident = jnp.zeros(incoming.shape[:2] + (2,) + incoming.shape[3:], jnp.float32)
    rim_parts = []
    for key_index in range(key_count):
        combined = incoming[:, :, 0, None] * keys[key_index, 0]
        for digit_index in range(1, incoming.shape[2]):
            combined = combined + incoming[:, :, digit_index, None] * keys[key_index, digit_index]
        product = reduce_mod(combined, modulus) * marks[:, :, key_index, None, None, None]
        rotated = jnp.roll(product, -amounts[key_index], axis=4)
        inside = position < columns - amounts[key_index]
        resident = resident + jnp.where(inside, rotated, 0.0)
        rim_parts.append(jnp.where(inside, 0.0, rotated))
    rim_sum = rim_parts[0]
    for extra in rim_parts[1:]:
        rim_sum = rim_sum + extra
    arrived = from_behind(rim_sum[..., columns - widest :], "limb", -1)
    resident = resident + jnp.pad(arrived, ((0, 0),) * 4 + ((columns - widest, 0),))
    returned = lax.all_to_all(resident, "grp", split_axis=0, concat_axis=0, tiled=True)
    gathered = jnp.einsum("hsc,hsplx->cplx", chooser, returned, precision=exact_mode)
    return reduce_mod(gathered, modulus) / modulus


def solution(mesh):
    in_specs = (
        P("grp", None, None, "limb"),
        P("grp", None, None, None, "limb"),
        P("grp", None),
        P(),
        P(),
    )
    out_specs = P("grp", None, None, "limb")
    return jax.shard_map(
        per_device, mesh=mesh, in_specs=in_specs, out_specs=out_specs, check_vma=False
    )
```

profile of v0, /device:TPU:6, one launch (start us, length us, event | category | flops | bytes accessed | tf_op | source)
XLA Modules:
  0.0 219.3 jit_solution(17316462651476829666)
XLA Ops:
  0.0 0.7 convert_element_type.18
  1.0 0.8 fusion.20
  1.8 10.3 %all-to-all-start.1 = ((f32[8,2,4]{2,1,0:T(2,128)}), f32[8,2,4]{2,1,0:T(2,128)S(1)}, u32[]{:S(2)}, u32[]{:S(2)}) async-start(f32[8,2,4]{2,1,0:T(2,128)} %fusion.20), calls=%async_computation.1 | async-start | bytes 16384 | tf_op jit(solution)/shard_map/all_to_all | solution.py:46
  12.1 4.3 %fusion.16 = f32[8,2,3,16,1024]{4,0,3,2,1:T(8,128)S(1)} fusion(f32[4,3,16,1024]{3,2,1,0:T(8,128)} %param.7, f32[8,4]{0,1:T(4,128)S(1)} %get-tuple-element.29, f32[8,4]{0,1:T(4,128)S(1)} %add_bitcast_fusion), kind=kOutput, calls=%fused_computation.40 | convolution fusion | flops 37748864 | bytes 3932416 | tf_op jit(solution)/shard_map/hsc,cjlx->hsjlx/dot_general | solution.py:41
  16.4 3.5 %copy.46 = f32[8,2,3,16,1024]{4,3,2,1,0:T(8,128)} copy(f32[8,2,3,16,1024]{4,0,3,2,1:T(8,128)S(1)} %fusion.16) | data formatting | bytes 6291456 | tf_op jit(solution)/shard_map/hsc,cjlx->hsjlx/dot_general | solution.py:41
  19.9 7.3 %all-to-all-start = ((f32[8,2,3,16,1024]{4,3,2,1,0:T(8,128)}), f32[8,2,3,16,1024]{4,3,2,1,0:T(8,128)S(1)}, u32[]{:S(2)}, u32[]{:S(2)}) async-start(f32[8,2,3,16,1024]{4,3,2,1,0:T(8,128)} %copy.46), calls=%async_computation | async-start | bytes 6291456 | tf_op jit(solution)/shard_map/all_to_all | solution.py:45
  27.3 0.7 fusion.37
  34.1 0.6 slice.122
  37.4 2.4 %slice_bitcast_fusion.14 = (f32[2,16,1024]{2,1,0:T(8,128)S(1)}, f32[2,16,1024]{2,1,0:T(8,128)}, f32[2,16,1024]{2,1,0:T(8,128)S(1)}, f32[2,16,1024]{2,1,0:T(8,128...) fusion(f32[4,3,2,16,1024]{4,3,2,1,0:T(8,128)} %param.8), kind=kLoop, calls=%fused_computation.55 | loop fusion | bytes 3145728 | tf_op jit(solution)/shard_map/mul | solution.py:50
  39.9 0.7 fusion.36
  40.6 0.8 copy.58
  41.4 0.7 copy.59
  42.0 0.8 copy.52
  42.9 1.4 copy.54
  44.3 0.7 copy.55
  45.0 1.3 copy.56
  46.3 1.3 copy.57
  47.6 52.8 %all-to-all-done = f32[8,2,3,16,1024]{4,3,2,1,0:T(8,128)S(1)} async-done(((f32[8,2,3,16,1024]{4,3,2,1,0:T(8,128)}), f32[8,2,3,16,1024]{4,3,2,1,0:T(8,128)S(1)}, u32[]{:S(2)}, u32[]{:S(2)}) %all-to-all-start) | async-done | bytes 3145760 | tf_op jit(solution)/shard_map/all_to_all | solution.py:45
  100.6 0.8 copy.49
  101.5 0.8 copy.48
  102.3 0.8 copy.47
  103.3 4.5 %fusion.7 = f32[8,2,2,16,1024]{4,1,3,2,0:T(2,128)S(1)} fusion(f32[16]{0:T(128)S(1)} %copy-done.12, f32[8,2]{1,0:T(8,128)S(1)} %copy-done.10, f32[2,16,1024]{2,1,0:T(8,128)S(1)} %copy-done.7, f32[2,16,1024]{2,1,0:T(8,128)S(1)} %copy-done.8, f32[2,16,1024]{2,1,0:T(8,128)S(1)} %copy-done.6, f32[8,2,16,1024]{3,1,2,0:T(2,128)S(1)} %copy.49, ...), kind=kLoop, calls=%fused_computation.23 | loop fusion | flops 8388608 | bytes 5636288 | tf_op jit(solution)/shard_map/mul | solution.py:53
  107.9 13.2 %fusion.4 = (f32[8,2,2,16,1024]{4,1,3,2,0:T(2,128)S(1)}, f32[8,2,2,16,1024]{4,1,3,2,0:T(2,128)S(1)}, f32[8,2,2,16,1024]{4,1,3,2,0:T(2,128)S(1)}) fusion(f32[16]{0:T(128)S(1)} %copy-done.12, f32[8,2]{1,0:T(8,128)S(1)} %copy.53, f32[2,16,1024]{2,1,0:T(8,128)S(1)} %copy-done.4, f32[8,2,16,1024]{3,1,2,0:T(2,128)S(1)} %copy.49, f32[2,16,1024]{2,1,0:T(8,128)S(1)} %copy-done.5, ...), kind=kLoop, calls=%fused_computation.20 | loop fusion | flops 25165824 | bytes 10617152 | tf_op jit(solution)/shard_map/mul | solution.py:53
  121.1 9.1 %fusion = (f32[8,2,2,16,1024]{4,1,3,2,0:T(2,128)S(1)}, f32[8,2,2,16,1024]{4,1,3,2,0:T(2,128)S(1)}) fusion(s32[]{:T(128)S(6)} %select_n.103, f32[8,2,2,16,1024]{4,1,3,2,0:T(2,128)S(1)} %fusion.7, s32[]{:T(128)S(6)} %select_n.97, f32[8,2,2,16,1024]{4,1,3,2,0:T(2,128)S(1)} %get-tuple-element.6), kind=kLoop, calls=%fused_computation.16 | loop fusion | flops 1048576 | bytes 8388616 | tf_op jit(solution)/shard_map/jit(_roll_dynamic)/concatenate | solution.py:54
  130.3 8.8 %fusion.1 = (f32[8,2,2,16,1024]{4,1,3,2,0:T(2,128)S(1)}, f32[8,2,2,16,1024]{4,1,3,2,0:T(2,128)S(1)}) fusion(s32[]{:T(128)S(6)} %select_n.101, f32[8,2,2,16,1024]{4,1,3,2,0:T(2,128)S(1)} %get-tuple-element.8, s32[]{:T(128)S(6)} %select_n.99, f32[8,2,2,16,1024]{4,1,3,2,0:T(2,128)S(1)} %get-tuple-element.7), kind=kLoop, calls=%fused_computation.17 | loop fusion | flops 1048576 | bytes 8388616 | tf_op jit(solution)/shard_map/jit(_roll_dynamic)/concatenate | solution.py:54
  139.2 1.9 fusion.13
  141.1 5.2 %collective-permute-start = (f32[8,2,2,16,512]{4,1,3,2,0:T(2,128)S(1)}, f32[8,2,2,16,512]{4,1,3,2,0:T(2,128)S(1)}, u32[]{:S(2)}, u32[]{:S(2)}) collective-permute-start(f32[8,2,2,16,512]{4,1,3,2,0:T(2,128)S(1)} %fusion.13), channel_id=1, source_target_pairs={{0,63},{1,0},{2,1},{3,2},{4,3},{5,4},{6,5},{7,6},{8,7},{9,8},{10,9... | collective-permute-start | bytes 3145736 | tf_op jit(solution)/shard_map/ppermute | solution.py:16
  146.3 12.3 %collective-permute-done = f32[8,2,2,16,512]{4,1,3,2,0:T(2,128)S(1)} collective-permute-done((f32[8,2,2,16,512]{4,1,3,2,0:T(2,128)S(1)}, f32[8,2,2,16,512]{4,1,3,2,0:T(2,128)S(1)}, u32[]{:S(2)}, u32[]{:S(2)}) %collective-permute-start) | collective-permute-done | bytes 1048608 | tf_op jit(solution)/shard_map/ppermute | solution.py:16
  158.6 4.4 %pad_add_fusion = f32[8,2,2,16,1024]{4,1,3,2,0:T(2,128)S(1)} fusion(f32[8,2,2,16,512]{4,1,3,2,0:T(2,128)S(1)} %collective-permute-done, f32[8,2,2,16,1024]{4,1,3,2,0:T(2,128)S(1)} %get-tuple-element.36, f32[8,2,2,16,1024]{4,1,3,2,0:T(2,128)S(1)} %get-tuple-element.34, f32[8,2,2,16,1024]{4,1,3,2,0:T(2,128)S(1)} %get-tuple-element.35, ...), kind=kLoop, calls=%fused_computation.26 | loop fusion | flops 4194304 | bytes 11538432 | tf_op jit(solution)/shard_map/add | solution.py:62
  163.1 52.7 %all_to_all.15 = f32[8,2,2,16,1024]{4,1,3,2,0:T(2,128)S(1)} all-to-all(f32[8,2,2,16,1024]{4,1,3,2,0:T(2,128)S(1)} %pad_add_fusion), channel_id=1, replica_groups=mesh['grp'=8,'limb'=64] {'grp'}, dimensions={0} | all-to-all | bytes 4194304 | tf_op jit(solution)/shard_map/all_to_all | solution.py:63
  215.7 2.4 %fusion.10 = f32[4,2,16,1024]{3,0,2,1:T(4,128)S(1)} fusion(f32[8,2,2,16,1024]{4,1,3,2,0:T(2,128)S(1)} %all_to_all.15, f32[8,4]{0,1:T(4,128)S(1)} %get-tuple-element.29, f32[8,4]{0,1:T(4,128)S(1)} %add_bitcast_fusion), kind=kOutput, calls=%fused_computation.29 | convolution fusion | flops 25165952 | bytes 2621696 | tf_op jit(solution)/shard_map/hsc,hsplx->cplx/dot_general | solution.py:64
  218.1 1.2 fusion.19
  (72 shorter events, 4.7 us)
Async XLA Ops:
  1.8 18.1 %all-to-all-start.1 = ((f32[8,2,4]{2,1,0:T(2,128)}), f32[8,2,4]{2,1,0:T(2,128)S(1)}, u32[]{:S(2)}, u32[]{:S(2)}) async-start(f32[8,2,4]{2,1,0:T(2,128)} %fusion.20), calls=%async_computation.1 | async-start | bytes 16384 | tf_op jit(solution)/shard_map/all_to_all | solution.py:46
  19.9 7.3 %copy-start.25 = (s32[32]{0:T(128)S(1)}, s32[32]{0:T(128)}, u32[]{:S(2)}) copy-start(s32[32]{0:T(128)} %param.10) | copy-start | bytes 388
  19.9 13.1 %copy-start.26 = (s32[16]{0:T(128)S(1)}, s32[16]{0:T(128)}, u32[]{:S(2)}) copy-start(s32[16]{0:T(128)} %param.11) | copy-start | bytes 196
  19.9 80.6 %all-to-all-start = ((f32[8,2,3,16,1024]{4,3,2,1,0:T(8,128)}), f32[8,2,3,16,1024]{4,3,2,1,0:T(8,128)S(1)}, u32[]{:S(2)}, u32[]{:S(2)}) async-start(f32[8,2,3,16,1024]{4,3,2,1,0:T(8,128)} %copy.46), calls=%async_computation | async-start | bytes 6291456 | tf_op jit(solution)/shard_map/all_to_all | solution.py:45
  33.5 0.6 copy-start.13
  33.5 1.2 copy-start.15
  35.2 0.6 copy-start.17
  35.2 1.2 copy-start.19
  101.5 1.7 copy-start.6
  101.5 1.7 copy-start.7
  101.5 1.7 copy-start.8
  101.5 1.7 copy-start.10
  101.5 1.7 copy-start.11
  101.5 1.7 copy-start.12
  103.2 4.6 %copy-start = (f32[2,16,1024]{2,1,0:T(8,128)S(1)}, f32[2,16,1024]{2,1,0:T(8,128)}, u32[]{:S(2)}) copy-start(f32[2,16,1024]{2,1,0:T(8,128)} %get-tuple-element.16) | copy-start | bytes 393220
  103.2 4.6 %copy-start.1 = (f32[2,16,1024]{2,1,0:T(8,128)S(1)}, f32[2,16,1024]{2,1,0:T(8,128)}, u32[]{:S(2)}) copy-start(f32[2,16,1024]{2,1,0:T(8,128)} %get-tuple-element.17) | copy-start | bytes 393220
  103.2 4.6 %copy-start.2 = (f32[2,16,1024]{2,1,0:T(8,128)S(1)}, f32[2,16,1024]{2,1,0:T(8,128)}, u32[]{:S(2)}) copy-start(f32[2,16,1024]{2,1,0:T(8,128)} %get-tuple-element.18) | copy-start | bytes 393220
  103.3 4.6 %copy-start.3 = (f32[2,16,1024]{2,1,0:T(8,128)S(1)}, f32[2,16,1024]{2,1,0:T(8,128)}, u32[]{:S(2)}) copy-start(f32[2,16,1024]{2,1,0:T(8,128)} %get-tuple-element.19) | copy-start | bytes 393220
  103.3 4.6 %copy-start.4 = (f32[2,16,1024]{2,1,0:T(8,128)S(1)}, f32[2,16,1024]{2,1,0:T(8,128)}, u32[]{:S(2)}) copy-start(f32[2,16,1024]{2,1,0:T(8,128)} %get-tuple-element.20) | copy-start | bytes 393220
  103.3 4.6 %copy-start.5 = (f32[2,16,1024]{2,1,0:T(8,128)S(1)}, f32[2,16,1024]{2,1,0:T(8,128)}, u32[]{:S(2)}) copy-start(f32[2,16,1024]{2,1,0:T(8,128)} %get-tuple-element.21) | copy-start | bytes 393220
  103.3 4.6 %copy-start.9 = (f32[8,2]{1,0:T(8,128)S(1)}, f32[8,2]{1,0:T(8,128)}, u32[]{:S(2)}) copy-start(f32[8,2]{1,0:T(8,128)} %copy.57) | copy-start | bytes 196
  130.2 8.9 %copy-start.21 = (pred[512]{0:T(512)(128)(4,1)S(1)}, pred[512]{0:T(512)(128)(4,1)}, u32[]{:S(2)}) copy-start(pred[512]{0:T(512)(128)(4,1)} %slice.122) | copy-start | bytes 1540
  130.2 8.9 %copy-start.22 = (pred[512]{0:T(512)(128)(4,1)S(1)}, pred[512]{0:T(512)(128)(4,1)}, u32[]{:S(2)}) copy-start(pred[512]{0:T(512)(128)(4,1)} %slice.120) | copy-start | bytes 1540
  130.2 8.9 %copy-start.23 = (pred[512]{0:T(512)(128)(4,1)S(1)}, pred[512]{0:T(512)(128)(4,1)}, u32[]{:S(2)}) copy-start(pred[512]{0:T(512)(128)(4,1)} %slice.118) | copy-start | bytes 1540
  130.2 8.9 %copy-start.24 = (pred[512]{0:T(512)(128)(4,1)S(1)}, pred[512]{0:T(512)(128)(4,1)}, u32[]{:S(2)}) copy-start(pred[512]{0:T(512)(128)(4,1)} %slice.116) | copy-start | bytes 1540
  139.1 19.5 %copy-start.14 = (pred[1024]{0:T(1024)(128)(4,1)S(1)}, pred[1024]{0:T(1024)(128)(4,1)}, u32[]{:S(2)}) copy-start(pred[1024]{0:T(1024)(128)(4,1)} %copy-done.13) | copy-start | bytes 3076
  139.2 19.5 %copy-start.16 = (pred[1024]{0:T(1024)(128)(4,1)S(1)}, pred[1024]{0:T(1024)(128)(4,1)}, u32[]{:S(2)}) copy-start(pred[1024]{0:T(1024)(128)(4,1)} %copy-done.15) | copy-start | bytes 3076
  139.2 19.5 %copy-start.18 = (pred[1024]{0:T(1024)(128)(4,1)S(1)}, pred[1024]{0:T(1024)(128)(4,1)}, u32[]{:S(2)}) copy-start(pred[1024]{0:T(1024)(128)(4,1)} %copy-done.17) | copy-start | bytes 3076
  139.2 19.5 %copy-start.20 = (pred[1024]{0:T(1024)(128)(4,1)S(1)}, pred[1024]{0:T(1024)(128)(4,1)}, u32[]{:S(2)}) copy-start(pred[1024]{0:T(1024)(128)(4,1)} %copy-done.19) | copy-start | bytes 3076
  141.1 17.5 %collective-permute-start = (f32[8,2,2,16,512]{4,1,3,2,0:T(2,128)S(1)}, f32[8,2,2,16,512]{4,1,3,2,0:T(2,128)S(1)}, u32[]{:S(2)}, u32[]{:S(2)}) collective-permute-start(f32[8,2,2,16,512]{4,1,3,2,0:T(2,128)S(1)} %fusion.13), channel_id=1, source_target_pairs={{0,63},{1,0},{2,1},{3,2},{4,3},{5,4},{6,5},{7,6},{8,7},{9,8},{10,9... | collective-permute-start | bytes 3145736 | tf_op jit(solution)/shard_map/ppermute | solution.py:16
where the time goes:
time: 220 us; the launch traced here: 219 us
  waiting for transfers between devices  65.1 us (30%)
  blocking collectives  52.7 us (24%)
  other arithmetic  45.2 us (21%)
  starting transfers between devices  22.9 us (10%)
  local copies, waits for them, and re-layouts  20.7 us (9%)
  matrix products  7.47 us (3%)
  between operations  5.41 us (2%)
    all_to_all x1, waiting for transfers between devices, per_device(): lax.all_to_all(outgoing, 'grp', split_axis=0, concat_axis=0, tiled=True)  52.8 us
    all_to_all x1, blocking collectives, per_device(): lax.all_to_all(resident, 'grp', split_axis=0, concat_axis=0, tiled=True)  52.7 us
    concatenate x2, other arithmetic, per_device(): rotated = jnp.roll(product, -amounts[key_index], axis=4)  17.9 us
    mul x2, other arithmetic, per_device(): reduce_mod(combined, modulus) * marks[:, :, key_index, None, None, None]  17.8 us
    ppermute x1, waiting for transfers between devices, from_behind(): return lax.ppermute(value, axis, pairs)  12.3 us
    all_to_all x1, starting transfers between devices, per_device(): lax.all_to_all(key_marks, 'grp', split_axis=0, concat_axis=0, tiled=True)  10.3 us
    all_to_all x1, starting transfers between devices, per_device(): lax.all_to_all(outgoing, 'grp', split_axis=0, concat_axis=0, tiled=True)  7.34 us
    ppermute x1, starting transfers between devices, from_behind(): return lax.ppermute(value, axis, pairs)  5.22 us
  transfers between devices with their start and end apart: 3, of which 2 were waited for; matrix products, arithmetic and copies ran while one was open for 10% of the time, Pallas kernels for 0%

commit v1 on v0

v1 whole, which is shorter than its diff:
```python
import jax
import jax.numpy as jnp
from jax import lax
from jax.experimental import pallas as pl
from jax.experimental.pallas import tpu as pltpu
from jax.sharding import PartitionSpec as P

MESH = pl.DeviceIdType.MESH
LINE = 4
HALF = 8
WIDE = 512


def reduce_mod(amount, modulus):
    quotient = jnp.floor(amount * (1.0 / modulus))
    remainder = amount - quotient * modulus
    remainder = jnp.where(remainder < 0, remainder + modulus, remainder)
    return jnp.where(remainder >= modulus, remainder - modulus, remainder)


def kernel(groups, limbs, rot, digits, keys, consts, out,
           dall, kall, fall, main, rim_out, part_in, rim_in,
           d_send, d_recv, f_send, f_recv, k_send, k_recv, r_send, r_recv,
           o_send, o_recv, d_local, k_local):
    z = lax.axis_index("grp")
    lb = lax.axis_index("limb")
    before = lax.rem(lb + limbs - 1, limbs)
    after = lax.rem(lb + 1, limbs)
    columns = digits.shape[-1]
    cts = digits.shape[0]
    nkeys = keys.shape[0]

    def zmod(value):
        return lax.rem(value, groups)

    def pos(a):
        return lax.rem(z + 2 * a, LINE)

    q0 = pos(0)
    ae = lax.rem((q0 + 1) // 2, 2)
    am = 1 - ae
    qe = pos(ae)
    he = qe // 2
    z_out = zmod(z + groups - 1 + 2 * he)
    z_far = zmod(z + groups - 2 + 4 * he)

    def own_digits(a, ct):
        return digits.at[ct, :, pl.ds(pl.multiple_of(HALF * a, HALF), HALF), :]

    def own_keys(a, key):
        return keys.at[key, :, :, pl.ds(pl.multiple_of(HALF * a, HALF), HALF), :]

    def remote(src, dst, send, recv, zt, lt):
        return pltpu.make_async_remote_copy(
            src_ref=src, dst_ref=dst, send_sem=send, recv_sem=recv,
            device_id=(zt, lt), device_id_type=MESH)

    def d_copy(a, d, ct, way, own=False):
        src = own_digits(a, ct) if own else dall.at[a, d, ct]
        return remote(src, dall.at[a, d, ct], d_send.at[a, way, d, ct], d_recv.at[a, d, ct],
                      zmod(z + 1 + (groups - 2) * way), lb)

    def f_copy(a, d, way):
        return remote(fall.at[a, d], fall.at[a, d], f_send.at[a, way, d], f_recv.at[a, d],
                      zmod(z + 1 + (groups - 2) * way), lb)

    def k_copy(a, key):
        q = pos(a)
        slot = 1 + 2 * lax.rem((q + 1) // 2, 2)
        return remote(own_keys(a, key), kall.at[a, slot, key], k_send.at[a, key],
                      k_recv.at[a, slot, key], zmod(z + groups - 1 + 2 * (q // 2)), lb)

    def k_forward(key):
        return remote(kall.at[ae, 3, key], kall.at[ae, 2, key], k_send.at[2, key],
                      k_recv.at[ae, 2, key], z_out, lb)

    def k_arrive(slot, key):
        remote(kall.at[ae, slot, key], kall.at[ae, slot, key], k_send.at[2, key],
               k_recv.at[ae, slot, key], z_out, lb).wait_recv()

    def r_copy(a, d, ct):
        return remote(rim_out.at[a, d, ct], rim_in.at[a, d, ct], r_send.at[a, d, ct],
                      r_recv.at[a, d, ct], z, before)

    def o_copy(a, way, d, ct):
        return remote(main.at[a, d, ct], part_in.at[a, way, d, ct], o_send.at[a, d, ct],
                      o_recv.at[a, way, d, ct], zmod(z + 1 + (groups - 2) * way), lb)

    def local_d(a, ct):
        return pltpu.make_async_copy(own_digits(a, ct), dall.at[a, pos(a), ct], d_local.at[a, ct])

    def local_k(a, key):
        return pltpu.make_async_copy(own_keys(a, key), kall.at[a, 0, key], k_local.at[a, key])

    def loop(count, body):
        lax.fori_loop(0, count, lambda i, c: (body(i), c)[1], 0)

    def compute(a, d, ct, slot, zg):
        flags = pltpu.roll(fall[a, d], lax.rem(256 - 32 * ct - nkeys * zg, 128), 1)
        m = jnp.concatenate([consts[1 + a]] * (columns // 128), axis=1)
        inv = jnp.concatenate([consts[3 + a]] * (columns // 128), axis=1)
        pad = jnp.zeros((HALF, WIDE), jnp.float32)
        for p in range(2):
            total = jnp.zeros((HALF, WIDE + columns), jnp.float32)
            for key in range(nkeys):
                x = dall[a, d, ct, 0] * kall[a, slot, key, 0, p]
                x = x + dall[a, d, ct, 1] * kall[a, slot, key, 1, p]
                x = x + dall[a, d, ct, 2] * kall[a, slot, key, 2, p]
                t = (x - jnp.floor(x * inv) * m) * flags[:, key:key + 1]
                shift = WIDE + columns - 2 * rot[nkeys * zg + key]
                total = total + pltpu.roll(jnp.concatenate([pad, t], axis=1), shift, 1)
            rim_out[a, d, ct, p] = rim_out[a, d, ct, p] + total[:, :WIDE]
            main[a, d, ct, p] = main[a, d, ct, p] + total[:, WIDE:]

    def start_local(i):
        local_d(i // cts, lax.rem(i, cts)).start()
        local_k(i // cts, lax.rem(i, cts)).start()
    loop(2 * cts, start_local)
    for a in range(2):
        fall[a, pos(a)] = consts[0]
    barrier = pltpu.get_barrier_semaphore()
    for zt, lt in ((zmod(z + 1), lb), (zmod(z + groups - 1), lb), (z, before), (z, after)):
        pl.semaphore_signal(barrier, inc=1, device_id=(zt, lt), device_id_type=MESH)
    pl.semaphore_wait(barrier, 4)

    for a in range(2):
        @pl.when(pos(a) < LINE - 1)
        def _():
            f_copy(a, pos(a), 0).start()

        @pl.when(pos(a) > 0)
        def _():
            f_copy(a, pos(a), 1).start()

    def send_own(i):
        a, ct = i // cts, lax.rem(i, cts)

        @pl.when(pos(a) < LINE - 1)
        def _():
            d_copy(a, pos(a), ct, 0, True).start()

        @pl.when(pos(a) > 0)
        def _():
            d_copy(a, pos(a), ct, 1, True).start()
    loop(2 * cts, send_own)
    loop(2 * nkeys, lambda i: k_copy(i // nkeys, lax.rem(i, nkeys)).start())

    def clear(i):
        a, d, ct = i // (LINE * cts), lax.rem(i // cts, LINE), lax.rem(i, cts)
        main[a, d, ct] = jnp.zeros(main.shape[3:], jnp.float32)
        rim_out[a, d, ct] = jnp.zeros(rim_out.shape[3:], jnp.float32)
    loop(2 * LINE * cts, clear)

    def wait_local(i):
        local_d(i // cts, lax.rem(i, cts)).wait()
        local_k(i // cts, lax.rem(i, cts)).wait()
    loop(2 * cts, wait_local)

    def own_block(i):
        a, ct = i // cts, lax.rem(i, cts)
        compute(a, pos(a), ct, 0, z)

        @pl.when(a == am)
        def _():
            r_copy(a, pos(a), ct).start()
    loop(2 * cts, own_block)

    def gathered(s, i, slots):
        way, ct, a = lax.rem(i, 2), lax.rem(i // 2, cts), i // (2 * cts)
        q = pos(a)
        d = q + (2 * way - 1) * s

        @pl.when((d >= 0) & (d < LINE))
        def _():
            d_copy(a, d, ct, way).wait_recv()
            onward = (1 - way) * (LINE - 1 - q) + way * q > 0

            @pl.when(onward)
            def _():
                d_copy(a, d, ct, way).start()

            @pl.when(ct == 0)
            def _():
                f_copy(a, d, way).wait_recv()

                @pl.when(onward)
                def _():
                    f_copy(a, d, way).start()

            if slots == 1:
                compute(a, d, ct, 0, z)
            else:
                ends = 1 - (a - ae) * (a - ae)

                def one(slot):
                    compute(a, d, ct, slot, z * (1 - slot) + z_out * slot)
                loop(1 + ends, one)

            @pl.when(a == am)
            def _():
                r_copy(a, d, ct).start()

    per_step = 4 * cts
    loop(per_step, lambda i: gathered(1, i, 1))

    def relay(key):
        k_arrive(3, key)
        k_forward(key).start()
    loop(nkeys, relay)
    loop(nkeys, lambda key: k_arrive(1, key))

    def near_keys(i):
        step, ct = i // cts, lax.rem(i, cts)
        compute(ae, qe + step * (1 - 2 * he), ct, 1, z_out)
    loop(2 * cts, near_keys)

    loop(2 * per_step, lambda i: gathered(2 + i // per_step, lax.rem(i, per_step), 2))
    loop(nkeys, lambda key: k_arrive(2, key))

    def add_rim(a, d, ct):
        r_copy(a, d, ct).wait_recv()
        main[a, d, ct, :, :, columns - WIDE:] = (
            main[a, d, ct, :, :, columns - WIDE:] + rim_in[a, d, ct])

    def add_part(a, way, d, ct):
        o_copy(a, way, d, ct).wait_recv()
        main[a, d, ct] = main[a, d, ct] + part_in[a, way, d, ct]

    def last_keys(step, ct):
        d = (LINE - 1 - step) * (1 - he) + step * he
        compute(ae, d, ct, 2, z_far)
        r_copy(ae, d, ct).start()

    def pass_on(step, i):
        way, ct, a = lax.rem(i, 2), lax.rem(i // 2, cts), i // (2 * cts)
        q = pos(a)
        d = (LINE - 1 - step) * (1 - way) + step * way

        @pl.when((d - q) * (1 - 2 * way) > 0)
        def _():
            add_rim(a, d, ct)

            @pl.when((1 - way) * q + way * (LINE - 1 - q) > 0)
            def _():
                add_part(a, way, d, ct)
            o_copy(a, way, d, ct).start()

    def tail(step):
        @pl.when(step < LINE)
        def _():
            loop(cts, lambda ct: last_keys(step, ct))

        @pl.when(step > 0)
        def _():
            loop(4 * cts, lambda i: pass_on(step - 1, i))
    loop(LINE, tail)

    def finish(i):
        a, ct = i // cts, lax.rem(i, cts)
        q = pos(a)
        add_rim(a, q, ct)

        @pl.when(q > 0)
        def _():
            add_part(a, 0, q, ct)

        @pl.when(q < LINE - 1)
        def _():
            add_part(a, 1, q, ct)
        out[ct, :, pl.ds(pl.multiple_of(HALF * a, HALF), HALF), :] = main[a, q, ct]
    loop(2 * cts, finish)

    def drain(i):
        a, d, ct = i // (LINE * cts), lax.rem(i // cts, LINE), lax.rem(i, cts)
        q = pos(a)
        r_copy(a, d, ct).wait_send()

        @pl.when((q < LINE - 1) & (d <= q))
        def _():
            d_copy(a, d, ct, 0).wait_send()

            @pl.when(ct == 0)
            def _():
                f_copy(a, d, 0).wait_send()

        @pl.when((q > 0) & (d >= q))
        def _():
            d_copy(a, d, ct, 1).wait_send()

            @pl.when(ct == 0)
            def _():
                f_copy(a, d, 1).wait_send()

        @pl.when((d < q) | (d > q))
        def _():
            o_copy(a, 0, d, ct).wait_send()
    loop(2 * LINE * cts, drain)
    loop(2 * nkeys, lambda i: k_copy(i // nkeys, lax.rem(i, nkeys)).wait_send())
    loop(nkeys, lambda key: k_forward(key).wait_send())


def per_device(digits, keys, requests, rotations, moduli):
    groups, limbs = lax.axis_size("grp"), lax.axis_size("limb")
    cts, dnum, limb_count, columns = digits.shape
    nkeys = keys.shape[0]
    modulus = moduli.astype(jnp.float32)
    flags = jnp.broadcast_to(requests.astype(jnp.float32).reshape(1, 1, 128), (1, HALF, 128))
    mods = jnp.broadcast_to(modulus.reshape(2, HALF, 1), (2, HALF, 128))
    consts = jnp.concatenate([flags, mods, 1.0 / mods], axis=0)
    f32 = jnp.float32
    dma = pltpu.SemaphoreType.DMA
    any_space = pl.BlockSpec(memory_space=pl.ANY)
    total = pl.pallas_call(
        lambda *refs: kernel(groups, limbs, *refs),
        out_shape=jax.ShapeDtypeStruct((cts, 2, limb_count, columns), f32),
        in_specs=[pl.BlockSpec(memory_space=pltpu.SMEM), any_space, any_space,
                  pl.BlockSpec(memory_space=pltpu.VMEM)],
        out_specs=pl.BlockSpec(memory_space=pltpu.VMEM),
        scratch_shapes=[
            pltpu.VMEM((2, LINE, cts, dnum, HALF, columns), f32),
            pltpu.VMEM((2, 4, nkeys, dnum, 2, HALF, columns), f32),
            pltpu.VMEM((2, LINE, HALF, 128), f32),
            pltpu.VMEM((2, LINE, cts, 2, HALF, columns), f32),
            pltpu.VMEM((2, LINE, cts, 2, HALF, WIDE), f32),
            pltpu.VMEM((2, 2, LINE, cts, 2, HALF, columns), f32),
            pltpu.VMEM((2, LINE, cts, 2, HALF, WIDE), f32),
            dma((2, 2, LINE, cts)), dma((2, LINE, cts)),
            dma((2, 2, LINE)), dma((2, LINE)),
            dma((3, nkeys)), dma((2, 4, nkeys)),
            dma((2, LINE, cts)), dma((2, LINE, cts)),
            dma((2, LINE, cts)), dma((2, 2, LINE, cts)),
            dma((2, cts)), dma((2, nkeys)),
        ],
        compiler_params=pltpu.CompilerParams(
            collective_id=0, has_side_effects=True, vmem_limit_bytes=60 * 1024 * 1024),
        name="keyswitch",
    )(rotations, digits, keys, consts)
    column = modulus[:, None]
    return reduce_mod(total, column) / column


def solution(mesh):
    in_specs = (
        P("grp", None, None, "limb"),
        P("grp", None, None, None, "limb"),
        P("grp", None),
        P(),
        P(),
    )
    out_specs = P("grp", None, None, "limb")
    return jax.shard_map(
        per_device, mesh=mesh, in_specs=in_specs, out_specs=out_specs, check_vma=False
    )
```

time: 220 us -> 157 us (0.71)
  Pallas kernels: 0 us -> 152 us
  waiting for transfers between devices: 65.1 us -> 0 us
  blocking collectives: 52.7 us -> 0 us
  other arithmetic: 45.2 us -> 4.14 us
  starting transfers between devices: 22.9 us -> 0 us
  local copies, waits for them, and re-layouts: 20.7 us -> 0.32 us
  matrix products: 7.47 us -> 0 us
  between operations: 5.41 us -> 0.03 us
    pallas_call x0 -> x1, Pallas kernels: none -> 152 us  [per_device(): pl.pallas_call(lambda *refs: kernel(groups, limbs, *refs), out_shape=jax....]
    all_to_all x2 -> x0, waiting for transfers between devices: 52.8 us -> none  [the longest x1 52.8 us: per_device(): lax.all_to_all(outgoing, 'grp', split_axis=0, concat_axis=0, tiled=True)]
    all_to_all x1 -> x0, blocking collectives: 52.7 us -> none  [per_device(): lax.all_to_all(resident, 'grp', split_axis=0, concat_axis=0, tiled=True)]
    mul x4 -> x0, other arithmetic: 17.8 us -> none  [the longest x2 17.8 us: per_device(): reduce_mod(combined, modulus) * marks[:, :, key_index, None, None, None]]
    all_to_all x2 -> x0, starting transfers between devices: 17.7 us -> none  [the longest x1 10.3 us: per_device(): lax.all_to_all(key_marks, 'grp', split_axis=0, concat_axis=0, tiled=True)]
    concatenate x2 -> x1, other arithmetic: 17.9 us -> 0.61 us  [per_device(): consts = jnp.concatenate([flags, mods, 1.0 / mods], axis=0)]
    ppermute x1 -> x0, waiting for transfers between devices: 12.3 us -> none  [from_behind(): return lax.ppermute(value, axis, pairs)]
    mul x10 -> x0, local copies, waits for them, and re-layouts: 8.02 us -> none  [the longest x3 3.48 us: per_device(): combined = incoming[:, :, 0, None] * keys[key_index, 0]]
  transfers between devices with their start and end apart: 3 -> 0, of which waited for: 2 -> 0; matrix products, arithmetic and copies ran while one was open for 10% -> 0% of each run, Pallas kernels for 0% -> 0%
where the time goes in v1:
time: 157 us; the launch traced here: 156 us
  Pallas kernels  152 us (97%)
  other arithmetic  4.14 us (3%)
    pallas_call x1, Pallas kernels, per_device(): pl.pallas_call(lambda *refs: kernel(groups, limbs, *refs), out_shape=jax....  152 us

profile of v1, /device:TPU:6, one launch (start us, length us, event | category | flops | bytes accessed | tf_op | source)
XLA Modules:
  0.0 156.1 jit_solution(14598658557408879034)
XLA Ops:
  0.0 0.0 copy-start
  0.0 0.7 convert_element_type.7
  0.7 0.1 broadcast_in_dim.20
  0.8 0.1 broadcast_in_dim.22
  0.9 0.1 broadcast_in_dim.21
  1.0 0.7 convert_element_type.6
  1.7 0.1 broadcast_in_dim.18
  1.7 0.6 pad_maximum_fusion.refs_3_
  2.4 151.6 %keyswitch.1 = f32[4,2,16,1024]{3,2,1,0:T(8,128)} custom-call(s32[32]{0:T(128)} %refs_0_.1, f32[4,3,16,1024]{3,2,1,0:T(8,128)} %refs_1_.1, f32[4,3,2,16,1024]{4,3,2,1,0:T(8,128)} %refs_2_.1, f32[5,8,128]{2,1,0:T(8,128)} %pad_maximum_fusion.refs_3_), custom_call_target="tpu_custom_call" | custom-call | tf_op jit(solution)/shard_map/keyswitch/pallas_call | solution.py:313
  153.9 0.0 copy-done
  154.0 2.1 %fusion = f32[4,2,16,1024]{3,2,1,0:T(8,128)} fusion(f32[4,2,16,1024]{3,2,1,0:T(8,128)} %keyswitch.1, f32[16]{0:T(128)S(1)} %convert_element_type.7, f32[16]{0:T(128)S(1)} %broadcast_divide_fusion.1), kind=kLoop, calls=%fused_computation.2 | loop fusion | flops 1441792 | bytes 1048704 | tf_op jit(solution)/shard_map/div | solution.py:339
  (3 shorter events, 0.0 us)
Async XLA Ops:
  0.0 153.9 %copy-start = (s32[16]{0:T(128)S(1)}, s32[16]{0:T(128)}, u32[]{:S(2)}) copy-start(s32[16]{0:T(128)} %param.9) | copy-start | bytes 196

commit v2 on v1

v2 whole, which is shorter than its diff:
```python
import jax
import jax.numpy as jnp
from jax import lax
from jax.experimental import pallas as pl
from jax.experimental.pallas import tpu as pltpu
from jax.sharding import PartitionSpec as P

MESH = pl.DeviceIdType.MESH
LINE = 4
HALF = 8
WIDE = 512
GROUP = 2


def reduce_mod(amount, modulus):
    quotient = jnp.floor(amount * (1.0 / modulus))
    remainder = amount - quotient * modulus
    remainder = jnp.where(remainder < 0, remainder + modulus, remainder)
    return jnp.where(remainder >= modulus, remainder - modulus, remainder)


def kernel(groups, limbs, rot, mods, digits, keys, requests, out,
           consts, flag, dall, kall, fall, main, rim_out, part_in, rim_in,
           d_send, d_recv, f_send, f_recv, k_send, k_recv, r_send, r_recv,
           o_send, o_recv, d_local, k_local):
    z = lax.axis_index("grp")
    lb = lax.axis_index("limb")
    before = lax.rem(lb + limbs - 1, limbs)
    after = lax.rem(lb + 1, limbs)
    columns = digits.shape[-1]
    cts = digits.shape[0]
    nkeys = keys.shape[0]

    def zmod(value):
        return lax.rem(value, groups)

    def pos(a):
        return lax.rem(z + 2 * a, LINE)

    q0 = pos(0)
    ae = lax.rem((q0 + 1) // 2, 2)
    am = 1 - ae
    qe = pos(ae)
    he = qe // 2
    z_out = zmod(z + groups - 1 + 2 * he)
    z_far = zmod(z + groups - 2 + 4 * he)

    parts = cts // GROUP

    def several(h):
        return pl.ds(GROUP * h, GROUP)

    def own_digits(a, h):
        return digits.at[several(h), :, pl.ds(pl.multiple_of(HALF * a, HALF), HALF), :]

    def own_keys(a, key):
        return keys.at[key, :, :, pl.ds(pl.multiple_of(HALF * a, HALF), HALF), :]

    def remote(src, dst, send, recv, zt, lt):
        return pltpu.make_async_remote_copy(
            src_ref=src, dst_ref=dst, send_sem=send, recv_sem=recv,
            device_id=(zt, lt), device_id_type=MESH)

    def d_copy(a, d, h, way, own=False):
        here = dall.at[a, d, several(h)]
        return remote(own_digits(a, h) if own else here, here, d_send.at[a, way, d, h],
                      d_recv.at[a, d, h], zmod(z + 1 + (groups - 2) * way), lb)

    def f_copy(a, d, way):
        return remote(fall.at[a, d], fall.at[a, d], f_send.at[a, way, d], f_recv.at[a, d],
                      zmod(z + 1 + (groups - 2) * way), lb)

    def k_copy(a, key):
        q = pos(a)
        slot = 1 + 2 * lax.rem((q + 1) // 2, 2)
        return remote(own_keys(a, key), kall.at[a, slot, key], k_send.at[a, key],
                      k_recv.at[a, slot, key], zmod(z + groups - 1 + 2 * (q // 2)), lb)

    def k_forward(key):
        return remote(kall.at[ae, 3, key], kall.at[ae, 2, key], k_send.at[2, key],
                      k_recv.at[ae, 2, key], z_out, lb)

    def k_arrive(slot, key):
        remote(kall.at[ae, slot, key], kall.at[ae, slot, key], k_send.at[2, key],
               k_recv.at[ae, slot, key], z_out, lb).wait_recv()

    def r_copy(a, d, h):
        return remote(rim_out.at[a, d, several(h)], rim_in.at[a, d, several(h)],
                      r_send.at[a, d, h], r_recv.at[a, d, h], z, before)

    def o_copy(a, way, d, h):
        return remote(main.at[a, d, several(h)], part_in.at[a, way, d, several(h)],
                      o_send.at[a, d, h], o_recv.at[a, way, d, h],
                      zmod(z + 1 + (groups - 2) * way), lb)

    def local_d(a, h):
        return pltpu.make_async_copy(own_digits(a, h), dall.at[a, pos(a), several(h)],
                                     d_local.at[a, h])

    def local_k(a, key):
        return pltpu.make_async_copy(own_keys(a, key), kall.at[a, 0, key], k_local.at[a, key])

    def loop(count, body):
        lax.fori_loop(0, count, lambda i, c: (body(i), c)[1], 0)

    def compute(a, d, ct, slot, zg):
        flags = pltpu.roll(fall[a, d], lax.rem(256 - 32 * ct - nkeys * zg, 128), 1)
        m = jnp.concatenate([consts[a]] * (columns // 128), axis=1)
        inv = jnp.concatenate([consts[2 + a]] * (columns // 128), axis=1)
        pad = jnp.zeros((HALF, WIDE), jnp.float32)
        for p in range(2):
            total = jnp.zeros((HALF, WIDE + columns), jnp.float32)
            for key in range(nkeys):
                x = dall[a, d, ct, 0] * kall[a, slot, key, 0, p]
                x = x + dall[a, d, ct, 1] * kall[a, slot, key, 1, p]
                x = x + dall[a, d, ct, 2] * kall[a, slot, key, 2, p]
                t = (x - jnp.floor(x * inv) * m) * flags[:, key:key + 1]
                shift = WIDE + columns - 2 * rot[nkeys * zg + key]
                total = total + pltpu.roll(jnp.concatenate([pad, t], axis=1), shift, 1)
            rim_out[a, d, ct, p] = rim_out[a, d, ct, p] + total[:, :WIDE]
            main[a, d, ct, p] = main[a, d, ct, p] + total[:, WIDE:]

    def compute_group(a, d, h, slot, zg):
        loop(GROUP, lambda c: compute(a, d, GROUP * h + c, slot, zg))

    loop(2 * parts, lambda i: local_d(i // parts, lax.rem(i, parts)).start())
    loop(2 * nkeys, lambda i: local_k(i // nkeys, lax.rem(i, nkeys)).start())
    barrier = pltpu.get_barrier_semaphore()
    for zt, lt in ((zmod(z + 1), lb), (zmod(z + groups - 1), lb), (z, before), (z, after)):
        pl.semaphore_signal(barrier, inc=1, device_id=(zt, lt), device_id_type=MESH)

    row = lax.broadcasted_iota(jnp.int32, (HALF, 128), 0)
    for a in range(2):
        m = jnp.ones((HALF, 128), jnp.float32)
        for limb in range(HALF):
            m = jnp.where(row == limb, mods[HALF * a + limb].astype(jnp.float32), m)
        consts[a] = m
        consts[2 + a] = 1.0 / m
    flag[...] = jnp.zeros_like(flag)
    flag[:cts, :requests.shape[1]] = requests[...].astype(jnp.float32)
    wanted = jnp.zeros((HALF, 128), jnp.float32)
    for ct in range(cts):
        spread = jnp.broadcast_to(flag[ct:ct + 1, :], (HALF, 128))
        wanted = wanted + pltpu.roll(spread, 32 * ct, 1)
    for a in range(2):
        fall[a, pos(a)] = wanted
    pl.semaphore_wait(barrier, 4)

    def send_own(i):
        a, h = i // parts, lax.rem(i, parts)

        @pl.when(pos(a) < LINE - 1)
        def _():
            d_copy(a, pos(a), h, 0, True).start()

        @pl.when(pos(a) > 0)
        def _():
            d_copy(a, pos(a), h, 1, True).start()
    loop(2 * parts, send_own)
    for a in range(2):
        @pl.when(pos(a) < LINE - 1)
        def _():
            f_copy(a, pos(a), 0).start()

        @pl.when(pos(a) > 0)
        def _():
            f_copy(a, pos(a), 1).start()
    loop(2 * nkeys, lambda i: k_copy(i // nkeys, lax.rem(i, nkeys)).start())

    def clear(i):
        a, d, ct = i // (LINE * cts), lax.rem(i // cts, LINE), lax.rem(i, cts)
        main[a, d, ct] = jnp.zeros(main.shape[3:], jnp.float32)
        rim_out[a, d, ct] = jnp.zeros(rim_out.shape[3:], jnp.float32)
    loop(2 * LINE * cts, clear)
    loop(2 * parts, lambda i: local_d(i // parts, lax.rem(i, parts)).wait())
    loop(2 * nkeys, lambda i: local_k(i // nkeys, lax.rem(i, nkeys)).wait())

    def own_block(i):
        a, h = i // parts, lax.rem(i, parts)
        compute_group(a, pos(a), h, 0, z)

        @pl.when(a == am)
        def _():
            r_copy(a, pos(a), h).start()
    loop(2 * parts, own_block)

    def gathered(s, i, slots):
        way, h, a = lax.rem(i, 2), lax.rem(i // 2, parts), i // (2 * parts)
        q = pos(a)
        d = q + (2 * way - 1) * s

        @pl.when((d >= 0) & (d < LINE))
        def _():
            d_copy(a, d, h, way).wait_recv()
            onward = (1 - way) * (LINE - 1 - q) + way * q > 0

            @pl.when(onward)
            def _():
                d_copy(a, d, h, way).start()

            @pl.when(h == 0)
            def _():
                f_copy(a, d, way).wait_recv()

                @pl.when(onward)
                def _():
                    f_copy(a, d, way).start()

            if slots == 1:
                compute_group(a, d, h, 0, z)
            else:
                ends = 1 - (a - ae) * (a - ae)

                def one(slot):
                    compute_group(a, d, h, slot, z * (1 - slot) + z_out * slot)
                loop(1 + ends, one)

            @pl.when(a == am)
            def _():
                r_copy(a, d, h).start()

    per_step = 4 * parts
    loop(per_step, lambda i: gathered(1, i, 1))

    def relay(key):
        k_arrive(3, key)
        k_forward(key).start()
    loop(nkeys, relay)
    loop(nkeys, lambda key: k_arrive(1, key))

    def near_keys(i):
        step, h = i // parts, lax.rem(i, parts)
        compute_group(ae, qe + step * (1 - 2 * he), h, 1, z_out)
    loop(2 * parts, near_keys)

    loop(2 * per_step, lambda i: gathered(2 + i // per_step, lax.rem(i, per_step), 2))
    loop(nkeys, lambda key: k_arrive(2, key))

    hm = pos(am) - 1

    def chain(way, item):
        return (LINE - 1 - item) * (1 - way) + item * way

    def add_rim(a, d, h):
        r_copy(a, d, h).wait_recv()
        at = several(h)
        main[a, d, at, :, :, columns - WIDE:] = (
            main[a, d, at, :, :, columns - WIDE:] + rim_in[a, d, at])

    def add_part(a, way, d, h):
        o_copy(a, way, d, h).wait_recv()
        main[a, d, several(h)] = main[a, d, several(h)] + part_in[a, way, d, several(h)]

    def pass_on(way, d, h):
        add_rim(am, d, h)
        add_part(am, way, d, h)
        o_copy(am, way, d, h).start()

    def tail(i):
        step, h = i // parts, lax.rem(i, parts)
        compute_group(ae, chain(he, step), h, 2, z_far)
        r_copy(ae, chain(he, step), h).start()

        @pl.when(step > 0)
        def _():
            d = chain(he, step - 1)
            add_rim(ae, d, h)
            o_copy(ae, he, d, h).start()

        @pl.when(step > 1)
        def _():
            pass_on(hm, chain(hm, step - 2), h)

        @pl.when(step > 2)
        def _():
            pass_on(1 - hm, (LINE - 1) * hm, h)
    loop(LINE * parts, tail)

    def finish(a, h):
        q = pos(a)
        at = several(h)
        add_rim(a, q, h)

        @pl.when(q > 0)
        def _():
            add_part(a, 0, q, h)

        @pl.when(q < LINE - 1)
        def _():
            add_part(a, 1, q, h)
        out[at, :, pl.ds(pl.multiple_of(HALF * a, HALF), HALF), :] = main[a, q, at]
    loop(parts, lambda h: finish(am, h))
    loop(parts, lambda h: finish(ae, h))

    def drain(i):
        a, d, h = i // (LINE * parts), lax.rem(i // parts, LINE), lax.rem(i, parts)
        q = pos(a)
        r_copy(a, d, h).wait_send()

        @pl.when((q < LINE - 1) & (d <= q))
        def _():
            d_copy(a, d, h, 0).wait_send()

            @pl.when(h == 0)
            def _():
                f_copy(a, d, 0).wait_send()

        @pl.when((q > 0) & (d >= q))
        def _():
            d_copy(a, d, h, 1).wait_send()

            @pl.when(h == 0)
            def _():
                f_copy(a, d, 1).wait_send()

        @pl.when((d < q) | (d > q))
        def _():
            o_copy(a, 0, d, h).wait_send()
    loop(2 * LINE * parts, drain)
    loop(2 * nkeys, lambda i: k_copy(i // nkeys, lax.rem(i, nkeys)).wait_send())
    loop(nkeys, lambda key: k_forward(key).wait_send())


def per_device(digits, keys, requests, rotations, moduli):
    groups, limbs = lax.axis_size("grp"), lax.axis_size("limb")
    cts, dnum, limb_count, columns = digits.shape
    nkeys = keys.shape[0]
    modulus = moduli.astype(jnp.float32)
    parts = cts // GROUP
    f32 = jnp.float32
    dma = pltpu.SemaphoreType.DMA
    smem = pl.BlockSpec(memory_space=pltpu.SMEM)
    vmem = pl.BlockSpec(memory_space=pltpu.VMEM)
    any_space = pl.BlockSpec(memory_space=pl.ANY)
    total = pl.pallas_call(
        lambda *refs: kernel(groups, limbs, *refs),
        out_shape=jax.ShapeDtypeStruct((cts, 2, limb_count, columns), f32),
        in_specs=[smem, smem, any_space, any_space, vmem],
        out_specs=vmem,
        scratch_shapes=[
            pltpu.VMEM((4, HALF, 128), f32),
            pltpu.VMEM((HALF, 128), f32),
            pltpu.VMEM((2, LINE, cts, dnum, HALF, columns), f32),
            pltpu.VMEM((2, 4, nkeys, dnum, 2, HALF, columns), f32),
            pltpu.VMEM((2, LINE, HALF, 128), f32),
            pltpu.VMEM((2, LINE, cts, 2, HALF, columns), f32),
            pltpu.VMEM((2, LINE, cts, 2, HALF, WIDE), f32),
            pltpu.VMEM((2, 2, LINE, cts, 2, HALF, columns), f32),
            pltpu.VMEM((2, LINE, cts, 2, HALF, WIDE), f32),
            dma((2, 2, LINE, parts)), dma((2, LINE, parts)),
            dma((2, 2, LINE)), dma((2, LINE)),
            dma((3, nkeys)), dma((2, 4, nkeys)),
            dma((2, LINE, parts)), dma((2, LINE, parts)),
            dma((2, LINE, parts)), dma((2, 2, LINE, parts)),
            dma((2, parts)), dma((2, nkeys)),
        ],
        compiler_params=pltpu.CompilerParams(
            collective_id=0, has_side_effects=True, vmem_limit_bytes=60 * 1024 * 1024),
        name="keyswitch",
    )(rotations, moduli, digits, keys, requests)
    column = modulus[:, None]
    return reduce_mod(total, column) / column


def solution(mesh):
    in_specs = (
        P("grp", None, None, "limb"),
        P("grp", None, None, None, "limb"),
        P("grp", None),
        P(),
        P(),
    )
    out_specs = P("grp", None, None, "limb")
    return jax.shard_map(
        per_device, mesh=mesh, in_specs=in_specs, out_specs=out_specs, check_vma=False
    )
```

time: 157 us -> 99.1 us (0.63)
  the two profiles are of different devices: /device:TPU:6 before, /device:TPU:1 now
where the time goes in v2:
time: 99.1 us; the launch traced here: 98.9 us
  Pallas kernels  95.5 us (96%)
  other arithmetic  3.41 us (3%)
    pallas_call x1, Pallas kernels, per_device(): pl.pallas_call(lambda *refs: kernel(groups, limbs, *refs), out_shape=jax....  95.5 us
    div x1, other arithmetic, per_device(): return reduce_mod(total, column) / column  2.09 us

profile of v2, /device:TPU:1, one launch (start us, length us, event | category | flops | bytes accessed | tf_op | source)
XLA Modules:
  0.0 98.9 jit_solution(7196827641654649908)
XLA Ops:
  0.0 0.7 broadcast_divide_fusion
  0.7 0.7 convert_element_type.3
  1.3 95.5 %keyswitch.1 = f32[4,2,16,1024]{3,2,1,0:T(8,128)} custom-call(s32[32]{0:T(128)} %refs_0_.1, s32[16]{0:T(128)} %refs_1_.1, f32[4,3,16,1024]{3,2,1,0:T(8,128)} %refs_2_.1, f32[4,3,2,16,1024]{4,3,2,1,0:T(8,128)} %refs_3_.1, s32[4,32]{1,0:T(4,128)} %refs_4_.1), custom_call_target="tpu_custom_call" | custom-call | tf_op jit(solution)/shard_map/keyswitch/pallas_call | solution.py:335
  96.8 2.1 %fusion = f32[4,2,16,1024]{3,2,1,0:T(8,128)} fusion(f32[4,2,16,1024]{3,2,1,0:T(8,128)} %keyswitch.1, f32[16]{0:T(128)S(1)} %convert_element_type.3, f32[16]{0:T(128)S(1)} %broadcast_divide_fusion), kind=kLoop, calls=%fused_computation.2 | loop fusion | flops 1441792 | bytes 1048704 | tf_op jit(solution)/shard_map/div | solution.py:362

commit v3 on v0

v3 whole, which is shorter than its diff:
```python
import jax
import jax.numpy as jnp
from jax import lax
from jax.experimental import pallas as pl
from jax.experimental.pallas import tpu as pltpu
from jax.sharding import PartitionSpec as P

MESH = pl.DeviceIdType.MESH
WIDE = 512
DEPTHS = 4
LIMBS = 4


def reduce_mod(amount, modulus):
    quotient = jnp.floor(amount * (1.0 / modulus))
    remainder = amount - quotient * modulus
    remainder = jnp.where(remainder < 0, remainder + modulus, remainder)
    return jnp.where(remainder >= modulus, remainder - modulus, remainder)


def place(r, c):
    return r * (r + 1) // 2 + c


CROSS = place(DEPTHS, 0)
SLOTS = CROSS + DEPTHS
LAST = DEPTHS - 1


def kernel(groups, limbs, rot, mods, digits, keys, requests, out,
           stage_d, stage_k, consts, flag, dbuf, kbuf, main, part_in, rim_out, rim_in,
           d_send, d_recv, k_send, k_recv, o_send, o_recv, r_send, r_recv, local):
    z = lax.axis_index("grp")
    lb = lax.axis_index("limb")
    before = lax.rem(lb + limbs - 1, limbs)
    after = lax.rem(lb + 1, limbs)
    cts, dnum = digits.shape[:2]
    nkeys = keys.shape[0]
    pages = cts * dnum
    rows = 2 * LIMBS
    f32 = jnp.float32

    def zmod(value):
        return lax.rem(value, groups)

    def side(r):
        return lax.rem(z + r, 2)

    def inward(r):
        return zmod(z + 1 + (groups - 2) * side(r))

    def outward(r):
        return zmod(z + groups - 1 + 2 * side(r))

    def quarter(r):
        at = r * (1 - side(r)) + (groups - 1 - r) * side(r)
        return zmod(at + groups - z) // 2

    sub = lax.broadcasted_iota(jnp.int32, (rows, WIDE), 0)
    lane = lax.broadcasted_iota(jnp.int32, (rows, WIDE), 1)
    low = sub < LIMBS

    def swap(x):
        return pltpu.roll(x, LIMBS, 0)

    def remote(src, dst, send, recv, zt, lt):
        return pltpu.make_async_remote_copy(
            src_ref=src, dst_ref=dst, send_sem=send, recv_sem=recv,
            device_id=(zt, lt), device_id_type=MESH)

    def d_copy(r, c):
        s = place(r, c)
        t = place(r + 1, c) if r < LAST else CROSS + c
        return remote(dbuf.at[s], dbuf.at[t], d_send.at[s], d_recv.at[t], inward(r), lb)

    def d_arrive(t):
        remote(dbuf.at[t], dbuf.at[t], d_send.at[0], d_recv.at[t], z, lb).wait_recv()

    def k_copy(r, c, p):
        s, t = place(r, c), place(r + 1, c)
        return remote(kbuf.at[s, p], kbuf.at[t, p], k_send.at[s, p], k_recv.at[t, p],
                      inward(r), lb)

    def k_arrive(r, c, p):
        t = place(r, c)
        remote(kbuf.at[t, p], kbuf.at[t, p], k_send.at[0, p], k_recv.at[t, p], z, lb).wait_recv()

    def view(ref, s, p, h):
        return ref.at[s, p] if h is None else ref.at[s, p, pl.ds(2 * h, 2)]

    def o_cross(c, p, h=None):
        s, t, e = CROSS + c, place(LAST, c), 0 if h is None else h
        return remote(view(main, s, p, h), view(part_in, t, p, h),
                      o_send.at[s, p, e], o_recv.at[t, p, e], inward(LAST), lb)

    def o_copy(r, c, p, h=None):
        s, t, e = place(r, c), place(r - 1, c), 0 if h is None else h
        return remote(view(main, s, p, h), view(part_in, t, p, h),
                      o_send.at[s, p, e], o_recv.at[t, p, e], outward(r), lb)

    def r_copy(s, p, h=None):
        e = 0 if h is None else h
        src, dst = rim_out.at[s, p], rim_in.at[s, p]
        if h is not None:
            src, dst = src.at[pl.ds(h, 1)], dst.at[pl.ds(h, 1)]
        return remote(src, dst, r_send.at[s, p, e], r_recv.at[s, p, e], z, before)

    def loop(count, body):
        lax.fori_loop(0, count, lambda i, c: (body(i), c)[1], 0)

    def tiled(x):
        return jnp.concatenate([x] * (WIDE // 128), axis=1)

    def unit(s, r, k, p, h=None):
        held = r * (r + 1) // 2 + k
        zk = zmod(z + groups + (k - r) * (1 - 2 * side(r)))
        m = tiled(consts[r])
        inv = tiled(consts[DEPTHS + r])

        def pair(h):
            flags = pltpu.roll(dbuf[s, pages, :, :128],
                               lax.rem(256 - 64 * h - nkeys * zk, 128), 1)
            rim = rim_out[s, p, h]
            for e in range(2):
                ct = 2 * h + e
                total = jnp.zeros((rows, WIDE), f32)
                inside = jnp.zeros((rows, WIDE), f32)
                for key in range(nkeys):
                    x = dbuf[s, dnum * ct] * kbuf[held, p, key, 0]
                    for j in range(1, dnum):
                        x = x + dbuf[s, dnum * ct + j] * kbuf[held, p, key, j]
                    wanted = flags[:, 32 * e + key:32 * e + key + 1]
                    t = (x - jnp.floor(x * inv) * m) * wanted
                    kept = WIDE - 2 * rot[nkeys * zk + key]
                    t = pltpu.roll(t, kept, 1)
                    total = total + t
                    inside = inside + jnp.where(lane < kept, t, 0.0)
                wrapped = total - inside
                turned = swap(wrapped)
                main[s, p, ct] = main[s, p, ct] + (inside + jnp.where(low, turned, 0.0))
                if e == 0:
                    rim = rim + jnp.where(low, 0.0, turned)
                else:
                    rim = rim + jnp.where(low, wrapped, 0.0)
            rim_out[s, p, h] = rim
        if h is None:
            loop(cts // 2, pair)
        else:
            pair(h)

    def both(body):
        loop(2, body)

    def rims(s):
        both(lambda p: r_copy(s, p).start())

    def add_rim(s, p, h=None):
        r_copy(s, p, h).wait_recv()

        def pair(h):
            rim = rim_in[s, p, h]
            main[s, p, 2 * h] = main[s, p, 2 * h] + jnp.where(low, 0.0, rim)
            main[s, p, 2 * h + 1] = main[s, p, 2 * h + 1] + jnp.where(low, 0.0, swap(rim))
        if h is None:
            loop(cts // 2, pair)
        else:
            pair(h)

    def add_part(s, p, h=None):
        whole = view(part_in, s, p, h)
        e = 0 if h is None else h
        remote(whole, whole, o_send.at[0, p, e], o_recv.at[s, p, e], z, lb).wait_recv()
        at = (s, p) if h is None else (s, p, pl.ds(2 * h, 2))
        main[at] = main[at] + part_in[at]

    copy_d = pltpu.make_async_copy(digits, stage_d, local.at[0])
    copy_k = pltpu.make_async_copy(keys, stage_k, local.at[1])
    copy_d.start()
    copy_k.start()
    barrier = pltpu.get_barrier_semaphore()
    for zt, lt in ((zmod(z + 1), lb), (zmod(z + groups - 1), lb), (z, before), (z, after)):
        pl.semaphore_signal(barrier, inc=1, device_id=(zt, lt), device_id_type=MESH)

    row = lax.broadcasted_iota(jnp.int32, (rows, 128), 0)
    flag[...] = jnp.zeros_like(flag)
    flag[:cts, :requests.shape[1]] = requests[...].astype(f32)
    wanted = jnp.zeros((rows, 128), f32)
    for ct in range(cts):
        wanted = wanted + pltpu.roll(jnp.broadcast_to(flag[ct:ct + 1, :], (rows, 128)), 32 * ct, 1)
    wanted = jnp.concatenate([wanted] + [jnp.zeros((rows, 128), f32)] * (WIDE // 128 - 1), axis=1)
    for r in range(DEPTHS):
        dbuf[place(r, r), pages] = wanted
        m = jnp.ones((rows, 128), f32)
        for limb in range(LIMBS):
            value = mods[LIMBS * quarter(r) + limb].astype(f32)
            m = jnp.where((row == limb) | (row == limb + LIMBS), value, m)
        consts[r] = m
        consts[DEPTHS + r] = 1.0 / m

    def folded(x, r):
        first = lax.rem(quarter(r), 2) == 0
        a, b = x[:, :WIDE], x[:, WIDE:]
        return jnp.where(low, jnp.where(first, a, swap(a)), jnp.where(first, swap(b), b))

    def tile(r):
        return pl.ds(pl.multiple_of(rows * (quarter(r) // 2), rows), rows)

    copy_d.wait()
    for r in range(DEPTHS):
        def fold_d(i):
            dbuf[place(r, r), i] = folded(stage_d[i // dnum, lax.rem(i, dnum), tile(r), :], r)
        loop(pages, fold_d)
    pl.semaphore_wait(barrier, 4)
    for r in (0, 1, 2, 3):
        d_copy(r, r).start()
    copy_k.wait()

    def fold_keys(r, p):
        def fold_k(i):
            key, j = i // dnum, lax.rem(i, dnum)
            kbuf[place(r, r), p, key, j] = folded(stage_k[key, j, p, tile(r), :], r)
        loop(nkeys * dnum, fold_k)
    for r, p in ((0, 0), (1, 0), (0, 1), (2, 0)):
        fold_keys(r, p)
        k_copy(r, r, p).start()
    for r, p in ((3, 0), (1, 1), (2, 1), (3, 1)):
        fold_keys(r, p)

    def clear(i):
        s, p = i // 2, lax.rem(i, 2)
        main[s, p] = jnp.zeros(main.shape[2:], f32)
        rim_out[s, p] = jnp.zeros(rim_out.shape[2:], f32)
    loop(2 * SLOTS, clear)

    def own(i):
        r, p = i // 2, lax.rem(i, 2)
        unit(r * (r + 3) // 2, r, r, p)
    loop(2 * DEPTHS, own)
    rims(place(0, 0))

    for r in range(DEPTHS - 1):
        d_arrive(place(r + 1, r))
        d_copy(r + 1, r).start()

    def from_next(i):
        r, p = 1 + i // 2, lax.rem(i, 2)
        unit(r * (r + 1) // 2 + r - 1, r, r, p)
    loop(2 * LAST, from_next)
    for r in range(1, DEPTHS):
        rims(place(r, r - 1))
    d_arrive(CROSS + LAST)
    both(lambda p: unit(CROSS + LAST, LAST, LAST, p))

    k_arrive(1, 0, 0)
    k_copy(1, 0, 0).start()
    k_arrive(2, 1, 0)
    k_copy(2, 1, 0).start()
    k_arrive(3, 2, 0)
    loop(LAST, lambda i: unit((i + 1) * (i + 4) // 2, i + 1, i, 0))
    r_copy(place(1, 1), 0).start()
    unit(CROSS + 3, LAST, 2, 0)

    d_arrive(place(2, 0))
    d_copy(2, 0).start()
    both(lambda p: unit(place(2, 0), 2, 2, p))
    rims(place(2, 0))
    k_arrive(2, 0, 0)
    k_copy(2, 0, 0).start()
    for r in (2, 1):
        k_copy(r, r, 1).start()
    k_arrive(1, 0, 1)
    k_copy(1, 0, 1).start()
    unit(place(2, 2), 2, 0, 0)
    r_copy(place(2, 2), 0).start()

    def cross_block(c):
        loop(3, lambda i: unit(CROSS + c, LAST, LAST - i, 0))
        unit(CROSS + c, LAST, LAST, 1)

    d_arrive(place(3, 1))
    d_copy(3, 1).start()
    both(lambda p: unit(place(3, 1), 3, 3, p))
    rims(place(3, 1))
    k_arrive(3, 1, 0)
    unit(place(3, 3), 3, 1, 0)
    unit(CROSS + 3, 3, 1, 0)
    d_arrive(CROSS + 2)
    cross_block(2)

    d_arrive(place(3, 0))
    d_copy(3, 0).start()
    both(lambda p: unit(place(3, 0), 3, 3, p))
    rims(place(3, 0))
    for c in (1, 0):
        k_arrive(2, c, 1)
        k_copy(2, c, 1).start()
    unit(place(1, 1), 1, 0, 1)
    r_copy(place(1, 1), 1).start()
    d_arrive(CROSS + 1)
    cross_block(1)
    loop(2, lambda k: unit(place(2, 2), 2, k, 1))
    r_copy(place(2, 2), 1).start()

    k_arrive(3, 0, 0)
    unit(place(3, 3), 3, 0, 0)
    r_copy(place(3, 3), 0).start()
    d_arrive(CROSS)
    cross_block(0)

    def last_keys(c):
        unit(CROSS + c, LAST, 0, 0)
        r_copy(CROSS + c, 0).start()

    def leave(c):
        add_rim(CROSS + c, 0)
        o_cross(c, 0).start()

    def middle_keys(k):
        unit(place(3, 3), 3, k, 1)
        loop(DEPTHS, lambda c: unit(CROSS + c, LAST, k, 1))

    def pass_on(r, p):
        for c in range(r):
            add_rim(place(r, c), p)
            if p == 0:
                add_part(place(r, c), p)
                o_copy(r, c, p).start()
            else:
                def half(h):
                    add_part(place(r, c), p, h)
                    o_copy(r, c, p, h).start()
                loop(2, half)

    loop(DEPTHS, last_keys)
    loop(DEPTHS, leave)
    k_arrive(3, 2, 1)
    middle_keys(2)
    pass_on(3, 0)
    k_arrive(3, 1, 1)
    middle_keys(1)

    k_arrive(3, 0, 1)

    def last_half(i):
        c, h = i // 2, lax.rem(i, 2)
        unit(CROSS + c, LAST, 0, 1, h)
        r_copy(CROSS + c, 1, h).start()
    loop(2 * DEPTHS, last_half)
    unit(place(3, 3), 3, 0, 1)
    r_copy(place(3, 3), 1).start()

    def leave_half(i):
        c, h = i // 2, lax.rem(i, 2)
        add_rim(CROSS + c, 1, h)
        o_cross(c, 1, h).start()
    loop(2 * DEPTHS, leave_half)
    pass_on(2, 0)

    def finish(r, p):
        s = place(r, r)
        add_rim(s, p)
        if p == 0:
            add_part(s, p)
        else:
            loop(2, lambda h: add_part(s, p, h))
        first = lax.rem(quarter(r), 2) == 0
        mine = low == first

        def one(ct):
            v = main[s, p, ct]
            a = jnp.where(first, v, swap(v))
            b = jnp.where(first, swap(v), v)
            out[ct, p, tile(r), :WIDE] = jnp.where(mine, a, out[ct, p, tile(r), :WIDE])
            out[ct, p, tile(r), WIDE:] = jnp.where(mine, b, out[ct, p, tile(r), WIDE:])
        loop(cts, one)

    pass_on(3, 1)
    pass_on(1, 0)
    for r in (3, 2, 1):
        finish(r, 0)
    pass_on(2, 1)
    finish(0, 0)
    finish(3, 1)
    pass_on(1, 1)
    for r in (2, 1, 0):
        finish(r, 1)

    def sent(copy):
        copy(0).wait_send()
        loop(2, lambda h: copy(1, h).wait_send())

    for r in range(DEPTHS):
        for c in range(r + 1):
            d_copy(r, c).wait_send()
            if r < LAST:
                both(lambda p: k_copy(r, c, p).wait_send())
            if c < r:
                sent(lambda *ph: o_copy(r, c, *ph))
    for c in range(DEPTHS):
        sent(lambda *ph: o_cross(c, *ph))
        sent(lambda *ph: r_copy(CROSS + c, *ph))
    loop(2 * CROSS, lambda i: r_copy(i // 2, lax.rem(i, 2)).wait_send())


def per_device(digits, keys, requests, rotations, moduli):
    groups, limbs = lax.axis_size("grp"), lax.axis_size("limb")
    cts, dnum, limb_count, columns = digits.shape
    nkeys = keys.shape[0]
    modulus = moduli.astype(jnp.float32)
    f32 = jnp.float32
    dma = pltpu.SemaphoreType.DMA
    smem = pl.BlockSpec(memory_space=pltpu.SMEM)
    vmem = pl.BlockSpec(memory_space=pltpu.VMEM)
    any_space = pl.BlockSpec(memory_space=pl.ANY)
    rows = 2 * LIMBS
    total = pl.pallas_call(
        lambda *refs: kernel(groups, limbs, *refs),
        out_shape=jax.ShapeDtypeStruct((cts, 2, limb_count, columns), f32),
        in_specs=[smem, smem, any_space, any_space, vmem],
        out_specs=vmem,
        scratch_shapes=[
            pltpu.VMEM(digits.shape, f32),
            pltpu.VMEM(keys.shape, f32),
            pltpu.VMEM((2 * DEPTHS, rows, 128), f32),
            pltpu.VMEM((rows, 128), f32),
            pltpu.VMEM((SLOTS, cts * dnum + 1, rows, WIDE), f32),
            pltpu.VMEM((CROSS, 2, nkeys, dnum, rows, WIDE), f32),
            pltpu.VMEM((SLOTS, 2, cts, rows, WIDE), f32),
            pltpu.VMEM((CROSS, 2, cts, rows, WIDE), f32),
            pltpu.VMEM((SLOTS, 2, cts // 2, rows, WIDE), f32),
            pltpu.VMEM((SLOTS, 2, cts // 2, rows, WIDE), f32),
            dma((CROSS,)), dma((SLOTS,)),
            dma((CROSS, 2)), dma((CROSS, 2)),
            dma((SLOTS, 2, 2)), dma((CROSS, 2, 2)),
            dma((SLOTS, 2, 2)), dma((SLOTS, 2, 2)),
            dma((2,)),
        ],
        compiler_params=pltpu.CompilerParams(
            collective_id=0, has_side_effects=True, vmem_limit_bytes=60 * 1024 * 1024),
        name="keyswitch",
    )(rotations, moduli, digits, keys, requests)
    column = modulus[:, None]
    return reduce_mod(total, column) / column


def solution(mesh):
    in_specs = (
        P("grp", None, None, "limb"),
        P("grp", None, None, None, "limb"),
        P("grp", None),
        P(),
        P(),
    )
    out_specs = P("grp", None, None, "limb")
    return jax.shard_map(
        per_device, mesh=mesh, in_specs=in_specs, out_specs=out_specs, check_vma=False
    )
```

time: 220 us -> 101 us (0.46)
  the two profiles are of different devices: /device:TPU:6 before, /device:TPU:1 now
where the time goes in v3:
time: 101 us
  Pallas kernels  97.4 us (96%)
  other arithmetic  3.41 us (3%)
    pallas_call x1, Pallas kernels, per_device(): pl.pallas_call(lambda *refs: kernel(groups, limbs, *refs), out_shape=jax....  97.4 us
    div x1, other arithmetic, per_device(): return reduce_mod(total, column) / column  2.09 us

profile of v3, /device:TPU:1, one launch (start us, length us, event | category | flops | bytes accessed | tf_op | source)
XLA Modules:
  0.0 100.8 jit_solution(5329233592947011678)
XLA Ops:
  0.0 0.7 broadcast_divide_fusion
  0.7 0.7 convert_element_type.3
  1.3 97.4 %keyswitch.1 = f32[4,2,16,1024]{3,2,1,0:T(8,128)} custom-call(s32[32]{0:T(128)} %refs_0_.1, s32[16]{0:T(128)} %refs_1_.1, f32[4,3,16,1024]{3,2,1,0:T(8,128)} %refs_2_.1, f32[4,3,2,16,1024]{4,3,2,1,0:T(8,128)} %refs_3_.1, s32[4,32]{1,0:T(4,128)} %refs_4_.1), custom_call_target="tpu_custom_call" | custom-call | tf_op jit(solution)/shard_map/keyswitch/pallas_call | solution.py:416
  98.7 2.1 %fusion = f32[4,2,16,1024]{3,2,1,0:T(8,128)} fusion(f32[4,2,16,1024]{3,2,1,0:T(8,128)} %keyswitch.1, f32[16]{0:T(128)S(1)} %convert_element_type.3, f32[16]{0:T(128)S(1)} %broadcast_divide_fusion), kind=kLoop, calls=%fused_computation.2 | loop fusion | flops 1441792 | bytes 1048704 | tf_op jit(solution)/shard_map/div | solution.py:443

commit v4 on v3

--- a/solution.py
+++ b/solution.py
@@ -220,10 +220,9 @@
             key, j = i // dnum, lax.rem(i, dnum)
             kbuf[place(r, r), p, key, j] = folded(stage_k[key, j, p, tile(r), :], r)
         loop(nkeys * dnum, fold_k)
-    for r, p in ((0, 0), (1, 0), (0, 1), (2, 0)):
-        fold_keys(r, p)
-        k_copy(r, r, p).start()
-    for r, p in ((3, 0), (1, 1), (2, 1), (3, 1)):
+    fold_keys(0, 0)
+    k_copy(0, 0, 0).start()
+    for r, p in ((1, 0), (2, 0), (3, 0), (0, 1), (1, 1), (2, 1), (3, 1)):
         fold_keys(r, p)
 
     def clear(i):
@@ -238,74 +237,66 @@
     loop(2 * DEPTHS, own)
     rims(place(0, 0))
 
-    for r in range(DEPTHS - 1):
-        d_arrive(place(r + 1, r))
-        d_copy(r + 1, r).start()
-
-    def from_next(i):
-        r, p = 1 + i // 2, lax.rem(i, 2)
+    def from_next(i, r0):
+        r, p = r0 + i // 2, lax.rem(i, 2)
         unit(r * (r + 1) // 2 + r - 1, r, r, p)
-    loop(2 * LAST, from_next)
-    for r in range(1, DEPTHS):
-        rims(place(r, r - 1))
-    d_arrive(CROSS + LAST)
-    both(lambda p: unit(CROSS + LAST, LAST, LAST, p))
-
+
+    def block(s):
+        both(lambda p: unit(s, LAST, LAST, p))
+        rims(s)
+
+    d_arrive(place(1, 0))
+    d_copy(1, 0).start()
+    k_copy(1, 1, 0).start()
+    d_arrive(place(2, 1))
+    d_copy(2, 1).start()
+    loop(4, lambda i: from_next(i, 1))
+    rims(place(1, 0))
+    rims(place(2, 1))
+    d_arrive(place(3, 2))
+    d_copy(3, 2).start()
+    block(place(3, 2))
     k_arrive(1, 0, 0)
     k_copy(1, 0, 0).start()
+    d_arrive(place(2, 0))
+    d_copy(2, 0).start()
+    k_copy(2, 2, 0).start()
+    d_arrive(CROSS + 3)
+    both(lambda p: unit(CROSS + 3, LAST, LAST, p))
+    both(lambda p: unit(place(2, 0), 2, 2, p))
+    rims(place(2, 0))
     k_arrive(2, 1, 0)
     k_copy(2, 1, 0).start()
-    k_arrive(3, 2, 0)
-    loop(LAST, lambda i: unit((i + 1) * (i + 4) // 2, i + 1, i, 0))
-    r_copy(place(1, 1), 0).start()
-    unit(CROSS + 3, LAST, 2, 0)
-
-    d_arrive(place(2, 0))
-    d_copy(2, 0).start()
-    both(lambda p: unit(place(2, 0), 2, 2, p))
-    rims(place(2, 0))
+    d_arrive(place(3, 1))
+    d_copy(3, 1).start()
+    block(place(3, 1))
+    d_arrive(CROSS + 2)
+    both(lambda p: unit(CROSS + 2, LAST, LAST, p))
+    d_arrive(place(3, 0))
+    d_copy(3, 0).start()
+    block(place(3, 0))
     k_arrive(2, 0, 0)
     k_copy(2, 0, 0).start()
-    for r in (2, 1):
+    for r in (0, 1, 2):
         k_copy(r, r, 1).start()
-    k_arrive(1, 0, 1)
-    k_copy(1, 0, 1).start()
-    unit(place(2, 2), 2, 0, 0)
+    unit(place(1, 1), 1, 0, 0)
+    r_copy(place(1, 1), 0).start()
+    loop(2, lambda k: unit(place(2, 2), 2, k, 0))
     r_copy(place(2, 2), 0).start()
+    for k in (2, 1):
+        k_arrive(3, k, 0)
+        unit(place(3, 3), LAST, k, 0)
+        loop(2, lambda c: unit(CROSS + 2 + c, LAST, k, 0))
 
     def cross_block(c):
         loop(3, lambda i: unit(CROSS + c, LAST, LAST - i, 0))
         unit(CROSS + c, LAST, LAST, 1)
-
-    d_arrive(place(3, 1))
-    d_copy(3, 1).start()
-    both(lambda p: unit(place(3, 1), 3, 3, p))
-    rims(place(3, 1))
-    k_arrive(3, 1, 0)
-    unit(place(3, 3), 3, 1, 0)
-    unit(CROSS + 3, 3, 1, 0)
-    d_arrive(CROSS + 2)
-    cross_block(2)
-
-    d_arrive(place(3, 0))
-    d_copy(3, 0).start()
-    both(lambda p: unit(place(3, 0), 3, 3, p))
-    rims(place(3, 0))
     for c in (1, 0):
-        k_arrive(2, c, 1)
-        k_copy(2, c, 1).start()
-    unit(place(1, 1), 1, 0, 1)
-    r_copy(place(1, 1), 1).start()
-    d_arrive(CROSS + 1)
-    cross_block(1)
-    loop(2, lambda k: unit(place(2, 2), 2, k, 1))
-    r_copy(place(2, 2), 1).start()
-
+        d_arrive(CROSS + c)
+        cross_block(c)
     k_arrive(3, 0, 0)
-    unit(place(3, 3), 3, 0, 0)
+    unit(place(3, 3), LAST, 0, 0)
     r_copy(place(3, 3), 0).start()
-    d_arrive(CROSS)
-    cross_block(0)
 
     def last_keys(c):
         unit(CROSS + c, LAST, 0, 0)
@@ -319,23 +310,34 @@
         unit(place(3, 3), 3, k, 1)
         loop(DEPTHS, lambda c: unit(CROSS + c, LAST, k, 1))
 
-    def pass_on(r, p):
-        for c in range(r):
-            add_rim(place(r, c), p)
-            if p == 0:
-                add_part(place(r, c), p)
-                o_copy(r, c, p).start()
-            else:
-                def half(h):
-                    add_part(place(r, c), p, h)
-                    o_copy(r, c, p, h).start()
-                loop(2, half)
+    def pass_on(r, c, p):
+        add_rim(place(r, c), p)
+        if p == 0:
+            add_part(place(r, c), p)
+            o_copy(r, c, p).start()
+        else:
+            def half(h):
+                add_part(place(r, c), p, h)
+                o_copy(r, c, p, h).start()
+            loop(2, half)
 
     loop(DEPTHS, last_keys)
+    k_arrive(1, 0, 1)
+    k_copy(1, 0, 1).start()
+    unit(place(1, 1), 1, 0, 1)
+    r_copy(place(1, 1), 1).start()
+    k_arrive(2, 1, 1)
+    k_copy(2, 1, 1).start()
     loop(DEPTHS, leave)
+    unit(place(2, 2), 2, 1, 1)
+    k_arrive(2, 0, 1)
+    k_copy(2, 0, 1).start()
+    unit(place(2, 2), 2, 0, 1)
+    r_copy(place(2, 2), 1).start()
     k_arrive(3, 2, 1)
     middle_keys(2)
-    pass_on(3, 0)
+    for c in range(LAST):
+        pass_on(3, c, 0)
     k_arrive(3, 1, 1)
     middle_keys(1)
 
@@ -353,8 +355,6 @@
         c, h = i // 2, lax.rem(i, 2)
         add_rim(CROSS + c, 1, h)
         o_cross(c, 1, h).start()
-    loop(2 * DEPTHS, leave_half)
-    pass_on(2, 0)
 
     def finish(r, p):
         s = place(r, r)
@@ -374,15 +374,22 @@
             out[ct, p, tile(r), WIDE:] = jnp.where(mine, b, out[ct, p, tile(r), WIDE:])
         loop(cts, one)
 
-    pass_on(3, 1)
-    pass_on(1, 0)
-    for r in (3, 2, 1):
-        finish(r, 0)
-    pass_on(2, 1)
+    pass_on(2, 0, 0)
+    loop(2, leave_half)
+    pass_on(2, 1, 0)
+    loop(2 * DEPTHS - 2, lambda i: leave_half(2 + i))
+    pass_on(3, 0, 1)
+    finish(3, 0)
+    pass_on(1, 0, 0)
+    pass_on(3, 1, 1)
+    finish(2, 0)
+    pass_on(2, 0, 1)
+    pass_on(3, 2, 1)
+    finish(1, 0)
+    pass_on(2, 1, 1)
+    pass_on(1, 0, 1)
     finish(0, 0)
-    finish(3, 1)
-    pass_on(1, 1)
-    for r in (2, 1, 0):
+    for r in (3, 2, 1, 0):
         finish(r, 1)
 
     def sent(copy):

time: 101 us -> 93 us (0.921)
  the two profiles are of different devices: /device:TPU:1 before, /device:TPU:6 now
where the time goes in v4:
time: 93 us; the launch traced here: 92.8 us
  Pallas kernels  89.4 us (96%)
  other arithmetic  3.41 us (4%)
    pallas_call x1, Pallas kernels, per_device(): pl.pallas_call(lambda *refs: kernel(groups, limbs, *refs), out_shape=jax....  89.4 us
    div x1, other arithmetic, per_device(): return reduce_mod(total, column) / column  2.09 us

profile of v4, /device:TPU:6, one launch (start us, length us, event | category | flops | bytes accessed | tf_op | source)
XLA Modules:
  0.0 92.8 jit_solution(2675186085932885093)
XLA Ops:
  0.0 0.7 broadcast_divide_fusion
  0.7 0.7 convert_element_type.3
  1.3 89.4 %keyswitch.1 = f32[4,2,16,1024]{3,2,1,0:T(8,128)} custom-call(s32[32]{0:T(128)} %refs_0_.1, s32[16]{0:T(128)} %refs_1_.1, f32[4,3,16,1024]{3,2,1,0:T(8,128)} %refs_2_.1, f32[4,3,2,16,1024]{4,3,2,1,0:T(8,128)} %refs_3_.1, s32[4,32]{1,0:T(4,128)} %refs_4_.1), custom_call_target="tpu_custom_call" | custom-call | tf_op jit(solution)/shard_map/keyswitch/pallas_call | solution.py:423
  90.7 2.1 %fusion = f32[4,2,16,1024]{3,2,1,0:T(8,128)} fusion(f32[4,2,16,1024]{3,2,1,0:T(8,128)} %keyswitch.1, f32[16]{0:T(128)S(1)} %convert_element_type.3, f32[16]{0:T(128)S(1)} %broadcast_divide_fusion), kind=kLoop, calls=%fused_computation.2 | loop fusion | flops 1441792 | bytes 1048704 | tf_op jit(solution)/shard_map/div | solution.py:450

commit v5 on v4

--- a/solution.py
+++ b/solution.py
@@ -9,13 +9,6 @@
 WIDE = 512
 DEPTHS = 4
 LIMBS = 4
-
-
-def reduce_mod(amount, modulus):
-    quotient = jnp.floor(amount * (1.0 / modulus))
-    remainder = amount - quotient * modulus
-    remainder = jnp.where(remainder < 0, remainder + modulus, remainder)
-    return jnp.where(remainder >= modulus, remainder - modulus, remainder)
 
 
 def place(r, c):
@@ -206,20 +199,20 @@
         return pl.ds(pl.multiple_of(rows * (quarter(r) // 2), rows), rows)
 
     copy_d.wait()
+    pl.semaphore_wait(barrier, 4)
     for r in range(DEPTHS):
-        def fold_d(i):
-            dbuf[place(r, r), i] = folded(stage_d[i // dnum, lax.rem(i, dnum), tile(r), :], r)
-        loop(pages, fold_d)
-    pl.semaphore_wait(barrier, 4)
-    for r in (0, 1, 2, 3):
+        def fold_d(ct):
+            for j in range(dnum):
+                dbuf[place(r, r), dnum * ct + j] = folded(stage_d[ct, j, tile(r), :], r)
+        loop(cts, fold_d)
         d_copy(r, r).start()
     copy_k.wait()
 
     def fold_keys(r, p):
-        def fold_k(i):
-            key, j = i // dnum, lax.rem(i, dnum)
-            kbuf[place(r, r), p, key, j] = folded(stage_k[key, j, p, tile(r), :], r)
-        loop(nkeys * dnum, fold_k)
+        def fold_k(key):
+            for j in range(dnum):
+                kbuf[place(r, r), p, key, j] = folded(stage_k[key, j, p, tile(r), :], r)
+        loop(nkeys, fold_k)
     fold_keys(0, 0)
     k_copy(0, 0, 0).start()
     for r, p in ((1, 0), (2, 0), (3, 0), (0, 1), (1, 1), (2, 1), (3, 1)):
@@ -365,9 +358,13 @@
             loop(2, lambda h: add_part(s, p, h))
         first = lax.rem(quarter(r), 2) == 0
         mine = low == first
+        m, inv = tiled(consts[r]), tiled(consts[DEPTHS + r])
 
         def one(ct):
             v = main[s, p, ct]
+            v = v - jnp.floor(v * inv) * m
+            v = jnp.where(v < 0, v + m, v)
+            v = jnp.where(v >= m, v - m, v) / m
             a = jnp.where(first, v, swap(v))
             b = jnp.where(first, swap(v), v)
             out[ct, p, tile(r), :WIDE] = jnp.where(mine, a, out[ct, p, tile(r), :WIDE])
@@ -413,14 +410,13 @@
     groups, limbs = lax.axis_size("grp"), lax.axis_size("limb")
     cts, dnum, limb_count, columns = digits.shape
     nkeys = keys.shape[0]
-    modulus = moduli.astype(jnp.float32)
     f32 = jnp.float32
     dma = pltpu.SemaphoreType.DMA
     smem = pl.BlockSpec(memory_space=pltpu.SMEM)
     vmem = pl.BlockSpec(memory_space=pltpu.VMEM)
     any_space = pl.BlockSpec(memory_space=pl.ANY)
     rows = 2 * LIMBS
-    total = pl.pallas_call(
+    return pl.pallas_call(
         lambda *refs: kernel(groups, limbs, *refs),
         out_shape=jax.ShapeDtypeStruct((cts, 2, limb_count, columns), f32),
         in_specs=[smem, smem, any_space, any_space, vmem],
@@ -446,8 +442,6 @@
             collective_id=0, has_side_effects=True, vmem_limit_bytes=60 * 1024 * 1024),
         name="keyswitch",
     )(rotations, moduli, digits, keys, requests)
-    column = modulus[:, None]
-    return reduce_mod(total, column) / column
 
 
 def solution(mesh):

time: 93 us -> 92.5 us (level)
  other arithmetic: 3.41 us -> 0 us
  local copies, waits for them, and re-layouts: 0 us -> 1.89 us
  Pallas kernels: 89.4 us -> 90.4 us
    div x2 -> x0, other arithmetic: 2.75 us -> none  [the longest x1 2.09 us: per_device(): return reduce_mod(total, column) / column]
    unnamed x0 -> x1, local copies, waits for them, and re-layouts: none -> 1.89 us
    pallas_call x1, Pallas kernels: 89.4 us -> 90.4 us  [per_device(): pl.pallas_call(lambda *refs: kernel(groups, limbs, *refs), out_shape=jax....]
where the time goes in v5:
time: 92.5 us; the launch traced here: 92.3 us
  Pallas kernels  90.4 us (98%)
  local copies, waits for them, and re-layouts  1.89 us (2%)
    pallas_call x1, Pallas kernels, per_device(): pl.pallas_call(lambda *refs: kernel(groups, limbs, *refs), out_shape=jax....  90.4 us
    unnamed x1, local copies, waits for them, and re-layouts  1.89 us

profile of v5, /device:TPU:6, one launch (start us, length us, event | category | flops | bytes accessed | tf_op | source)
XLA Modules:
  0.0 92.3 jit_solution(8916877451813165284)
XLA Ops:
  0.0 90.4 %keyswitch.1 = f32[4,2,16,1024]{3,2,1,0:T(8,128)} custom-call(s32[32]{0:T(128)} %refs_0_.1, s32[16]{0:T(128)} %refs_1_.1, f32[4,3,16,1024]{3,2,1,0:T(8,128)} %refs_2_.1, f32[4,3,2,16,1024]{4,3,2,1,0:T(8,128)} %refs_3_.1, s32[4,32]{1,0:T(4,128)} %refs_4_.1), custom_call_target="tpu_custom_call" | custom-call | tf_op jit(solution)/shard_map/keyswitch/pallas_call | solution.py:419
  90.4 1.9 %copy.7 = f32[4,2,16,1024]{3,2,1,0:T(8,128)} copy(f32[4,2,16,1024]{3,2,1,0:T(8,128)} %keyswitch.1) | data formatting | bytes 1048576

commit v6 on v5

--- a/solution.py
+++ b/solution.py
@@ -304,8 +304,8 @@
         loop(DEPTHS, lambda c: unit(CROSS + c, LAST, k, 1))
 
     def pass_on(r, c, p):
-        add_rim(place(r, c), p)
         if p == 0:
+            add_rim(place(r, c), p)
             add_part(place(r, c), p)
             o_copy(r, c, p).start()
         else:
@@ -334,6 +334,9 @@
     k_arrive(3, 1, 1)
     middle_keys(1)
 
+    for r in range(1, DEPTHS):
+        for c in range(r):
+            add_rim(place(r, c), 1)
     k_arrive(3, 0, 1)
 
     def last_half(i):

time: 92.5 us -> 92.6 us (level)
  no operation moved by 1% of the time
where the time goes in v6:
time: 92.6 us; the launch traced here: 92.4 us
  Pallas kernels  90.5 us (98%)
  local copies, waits for them, and re-layouts  1.89 us (2%)
    pallas_call x1, Pallas kernels, per_device(): pl.pallas_call(lambda *refs: kernel(groups, limbs, *refs), out_shape=jax....  90.5 us
    unnamed x1, local copies, waits for them, and re-layouts  1.89 us

profile of v6, /device:TPU:6, one launch (start us, length us, event | category | flops | bytes accessed | tf_op | source)
XLA Modules:
  0.0 92.4 jit_solution(14718565009553925511)
XLA Ops:
  0.0 90.5 %keyswitch.1 = f32[4,2,16,1024]{3,2,1,0:T(8,128)} custom-call(s32[32]{0:T(128)} %refs_0_.1, s32[16]{0:T(128)} %refs_1_.1, f32[4,3,16,1024]{3,2,1,0:T(8,128)} %refs_2_.1, f32[4,3,2,16,1024]{4,3,2,1,0:T(8,128)} %refs_3_.1, s32[4,32]{1,0:T(4,128)} %refs_4_.1), custom_call_target="tpu_custom_call" | custom-call | tf_op jit(solution)/shard_map/keyswitch/pallas_call | solution.py:422
  90.5 1.9 %copy.7 = f32[4,2,16,1024]{3,2,1,0:T(8,128)} copy(f32[4,2,16,1024]{3,2,1,0:T(8,128)} %keyswitch.1) | data formatting | bytes 1048576
